TPU v7x, 32 devices: a whole 2x2x4 slice. The times are simulated.
32 devices in a mesh: rep: 2 (over x), px: 4 (over y, core), py: 4 (over z).
Axes of the slice: x: 2, y: 2, z: 4, core: 2. Of those that a mesh axis runs over, the one named last changes fastest.
Arguments:
- density: float32 [4, 128, 128, 128], P('rep', 'px', 'py'), parts along dimension 0, may hold values from -6 to 6
- kernel_factors: float32 [3, 89, 256], replicated, as said below
Outputs:
- potential: float32 [4, 128, 128, 128], P('rep', 'px', 'py'), parts along dimension 0
There are 2 independent parts, one for each index of `rep`. A program takes and returns all parts, laid end to end along the dimension named above; an argument that names none is the same for every part. Nothing has to cross between parts.
Inputs may be any that keep to these rules, and one draw needn't show every extreme that they name: Each factor is even in its frequency, kernel_factors[d, g, k] = kernel_factors[d, g, 256 - k], and is zero at k = 128.
All inputs are finite; a program needn't handle non-finite values.
Results may differ from a plain program's by a relative error of at most 0.00005.
Values sent between devices are 32-bit elements; how exact they have to be, the bound alone decides.
A program may use at most 128 MiB of HBM per device.

v0:
```python
import math

import jax
import jax.numpy as jnp
from jax import lax
from jax.sharding import PartitionSpec as P


def phases(out_index, in_index, period):
    product = out_index[:, None] * in_index[None, :] % period
    return product.astype(jnp.float32) * (2.0 * math.pi / period)


def along_last(table, values):
    return jnp.einsum(
        "kl,abl->kab",
        table,
        values,
        precision=lax.Precision.HIGHEST,
        preferred_element_type=jnp.float32,
    )


def along_first(values, table):
    return jnp.einsum(
        "kab,kl->abl",
        values,
        table,
        precision=lax.Precision.HIGHEST,
        preferred_element_type=jnp.float32,
    )


def forward_table(length, period, count):
    angles = phases(jnp.arange(count, dtype=jnp.int32), jnp.arange(length, dtype=jnp.int32), period)
    return jnp.concatenate([jnp.cos(angles), jnp.sin(angles)], 0)


def inverse_table(length, period):
    angles = phases(
        jnp.arange(period, dtype=jnp.int32), jnp.arange(length, dtype=jnp.int32), period
    )
    return jnp.concatenate([jnp.cos(angles), jnp.sin(angles)], 1)


def forward_pair(table, real_part, imag_part):
    count = table.shape[0] // 2
    from_real = along_last(table, real_part)
    from_imag = along_last(table, imag_part)
    return (from_real[:count] + from_imag[count:], from_imag[:count] - from_real[count:])


def inverse_pair(table, real_part, imag_part):
    length = table.shape[1] // 2
    from_real = along_first(real_part, table)
    from_imag = along_first(imag_part, table)
    return (
        from_real[..., :length] - from_imag[..., length:],
        from_real[..., length:] + from_imag[..., :length],
    )


def kernel_block(kernel_factors, y_start, y_count, z_start, z_count):
    terms = kernel_factors.shape[1]
    period = kernel_factors.shape[2]
    factor_y = lax.dynamic_slice_in_dim(kernel_factors[1], y_start, y_count, 1)
    factor_z = lax.dynamic_slice_in_dim(kernel_factors[2], z_start, z_count, 1)
    pair_yz = (factor_y[:, :, None] * factor_z[:, None, :]).reshape(terms, y_count * z_count)
    kernel = jnp.einsum("gx,gq->xq", kernel_factors[0], pair_yz, precision=lax.Precision.HIGHEST)
    return kernel.reshape(period, y_count, z_count)


def body(density, kernel_factors):
    replicas = density.shape[0]
    length = density.shape[3]
    period = 2 * length
    count_px = lax.axis_size("px")
    count_py = lax.axis_size("py")
    index_px = lax.axis_index("px")
    index_py = lax.axis_index("py")
    z_weights = jnp.where(jnp.arange(length, dtype=jnp.int32) == 0, 1.0, 2.0).astype(jnp.float32)
    real_table = forward_table(length, period, length)
    complex_table = forward_table(length, period, period)
    back_table = inverse_table(length, period)
    parts = []
    for replica in range(replicas):
        projected = along_last(real_table, density[replica])
        parts.append(projected[:length])
        parts.append(-projected[length:])
    parts = lax.all_to_all(tuple(parts), "py", split_axis=0, concat_axis=2, tiled=True)
    parts = list(parts)
    for replica in range(replicas):
        parts[2 * replica], parts[2 * replica + 1] = forward_pair(
            complex_table, parts[2 * replica], parts[2 * replica + 1]
        )
    parts = list(lax.all_to_all(tuple(parts), "px", split_axis=0, concat_axis=2, tiled=True))
    y_rows = period // count_px
    z_rows = length // count_py
    kernel = kernel_block(kernel_factors, index_px * y_rows, y_rows, index_py * z_rows, z_rows)
    for replica in range(replicas):
        real_part, imag_part = forward_pair(
            complex_table, parts[2 * replica], parts[2 * replica + 1]
        )
        parts[2 * replica], parts[2 * replica + 1] = inverse_pair(
            back_table, real_part * kernel, imag_part * kernel
        )
    parts = list(lax.all_to_all(tuple(parts), "px", split_axis=2, concat_axis=0, tiled=True))
    for replica in range(replicas):
        parts[2 * replica], parts[2 * replica + 1] = inverse_pair(
            back_table, parts[2 * replica], parts[2 * replica + 1]
        )
    parts = list(lax.all_to_all(tuple(parts), "py", split_axis=2, concat_axis=0, tiled=True))
    angles = phases(
        jnp.arange(length, dtype=jnp.int32), jnp.arange(length, dtype=jnp.int32), period
    )
    scaled = (z_weights * (1.0 / float(period) ** 3))[:, None]
    cos_table = jnp.cos(angles) * scaled
    sine_table = -jnp.sin(angles) * scaled
    results = []
    for replica in range(replicas):
        field = along_first(parts[2 * replica], cos_table) + along_first(
            parts[2 * replica + 1], sine_table
        )
        results.append(field)
    return jnp.stack(results, 0)


def solution(mesh):
    placed = (P("rep", "px", "py", None), P())
    return jax.shard_map(
        body, mesh=mesh, in_specs=placed, out_specs=P("rep", "px", "py", None), check_vma=False
    )
```

profile of v0, /device:TPU:0, one launch (start us, length us, event | category | flops | bytes accessed | tf_op | source)
XLA Modules:
  0.0 455.2 jit_solution(6071990530349432436)
XLA Ops:
  5.9 6.3 %all-to-all-start.9 = ((f32[4,1,32768]{2,1,0:T(1,128)}), f32[4,1,32768]{2,1,0:T(1,128)S(1)}, u32[]{:S(2)}, u32[]{:S(2)}) async-start(f32[4,1,32768]{2,1,0:T(1,128)} %reshape.34), calls=%async_computation.9 | async-start | bytes 1048576 | tf_op jit(solution)/shard_map/all_to_all | solution.py:90
  15.7 11.0 %all-to-all-done.9 = f32[4,1,32768]{2,1,0:T(1,128)S(1)} async-done(((f32[4,1,32768]{2,1,0:T(1,128)}), f32[4,1,32768]{2,1,0:T(1,128)S(1)}, u32[]{:S(2)}, u32[]{:S(2)}) %all-to-all-start.9) | async-done | bytes 524320 | tf_op jit(solution)/shard_map/all_to_all | solution.py:90
  26.8 3.5 all-to-all-start.8
  37.9 6.3 %all-to-all-done.8 = f32[4,1,32768]{2,1,0:T(1,128)S(1)} async-done(((f32[4,1,32768]{2,1,0:T(1,128)}), f32[4,1,32768]{2,1,0:T(1,128)S(1)}, u32[]{:S(2)}, u32[]{:S(2)}) %all-to-all-start.8) | async-done | bytes 524320 | tf_op jit(solution)/shard_map/all_to_all | solution.py:90
  45.1 3.6 all-to-all-start.1
  53.3 3.0 reduce.5
  57.1 3.1 copy.217
  60.2 3.1 all_to_all.247
  66.2 3.1 copy.218
  71.9 5.1 %all-to-all-start = ((f32[4,1,32768]{2,1,0:T(1,128)}), f32[4,1,32768]{2,1,0:T(1,128)S(1)}, u32[]{:S(2)}, u32[]{:S(2)}) async-start(f32[4,1,32768]{2,1,0:T(1,128)} %reshape.52), calls=%async_computation | async-start | bytes 1048576 | tf_op jit(solution)/shard_map/all_to_all | solution.py:90
  81.0 4.4 copy.172
  85.4 4.8 %reshape.40 = f32[4,1,65536]{2,1,0:T(1,128)} reshape(f32[256,32,32]{2,1,0:T(8,128)} %copy.172) | data formatting | bytes 2097152
  91.3 3.5 all-to-all-start.11
  94.8 4.4 copy.169
  99.2 4.9 %reshape.38 = f32[4,1,65536]{2,1,0:T(1,128)} reshape(f32[256,32,32]{2,1,0:T(8,128)} %copy.169) | data formatting | bytes 2097152
  108.9 3.1 copy.219
  112.0 3.1 all_to_all.215
  119.8 3.1 copy.220
  125.7 3.5 all-to-all-start.10
  134.2 5.3 %copy.143 = f32[256,32,32]{2,1,0:T(8,128)} copy(f32[256,32,32]{0,2,1:T(8,128)} %get-tuple-element.12) | data formatting | bytes 2097152 | tf_op jit(solution)/shard_map/add | solution.py:50
  139.6 4.8 %reshape.54 = f32[4,1,65536]{2,1,0:T(1,128)} reshape(f32[256,32,32]{2,1,0:T(8,128)} %copy.143) | data formatting | bytes 2097152
  144.4 4.4 all-to-all-start.2
  153.1 4.0 fusion.26
  157.1 4.4 copy.146
  161.5 4.8 %reshape.56 = f32[4,1,65536]{2,1,0:T(1,128)} reshape(f32[256,32,32]{2,1,0:T(8,128)} %copy.146) | data formatting | bytes 2097152
  166.3 3.7 reduce.7
  170.0 3.4 reshape.41
  173.4 3.5 copy.173
  176.9 4.5 all-to-all-start.3
  181.5 5.0 %fusion.78 = f32[512,64,32]{0,1,2:T(8,128)} fusion(f32[64,32,128]{0,2,1:T(8,128)S(1)} %bitcast.158, f32[256,128]{1,0:T(8,128)S(1)} %get-tuple-element.31, f32[256,128]{1,0:T(8,128)S(1)} %get-tuple-element.32), kind=kOutput, calls=%fused_computation.113 | convolution fusion | flops 1610678272 | bytes 5505024 | tf_op jit(solution)/shard_map/kl,abl->kab/dot_general | solution.py:15
  186.5 3.7 reduce.6
  190.1 3.4 reshape.39
  193.6 3.5 copy.170
  197.1 4.6 %reduce.3 = f32[4,65536]{1,0:T(4,128)S(1)} reduce(f32[4,1,65536]{2,1,0:T(1,128)} %all-to-all-done.2, f32[]{:T(128)} %broadcast.92), dimensions={1}, to_apply=%all_to_all.216.reduce_sub_computation | reduce | bytes 2097156 | tf_op jit(solution)/shard_map/all_to_all | solution.py:96
  201.7 3.4 reshape.55
  205.2 5.0 %copy.144 = f32[4,64,32,32]{1,3,0,2:T(8,128)} copy(f32[4,64,32,32]{3,2,1,0:T(8,128)} %bitcast.156) | data formatting | bytes 2097152 | tf_op jit(solution)/shard_map/all_to_all | solution.py:96
  210.2 5.1 %fusion.79 = f32[512,64,32]{0,1,2:T(8,128)} fusion(f32[64,32,128]{0,2,1:T(8,128)S(1)} %bitcast.159, f32[256,128]{1,0:T(8,128)S(1)} %get-tuple-element.31, f32[256,128]{1,0:T(8,128)S(1)} %get-tuple-element.32), kind=kOutput, calls=%fused_computation.114 | convolution fusion | flops 1610678272 | bytes 5505024 | tf_op jit(solution)/shard_map/kl,abl->kab/dot_general | solution.py:15
  215.3 5.1 %fusion.83 = f32[512,64,32]{0,1,2:T(8,128)} fusion(f32[64,32,128]{0,2,1:T(8,128)S(1)} %bitcast.160, f32[256,128]{1,0:T(8,128)S(1)} %get-tuple-element.31, f32[256,128]{1,0:T(8,128)S(1)} %get-tuple-element.32), kind=kOutput, calls=%fused_computation.118 | convolution fusion | flops 1610678272 | bytes 5505024 | tf_op jit(solution)/shard_map/kl,abl->kab/dot_general | solution.py:15
  220.4 4.6 %reduce.2 = f32[4,65536]{1,0:T(4,128)S(1)} reduce(f32[4,1,65536]{2,1,0:T(1,128)} %all-to-all-done.3, f32[]{:T(128)} %broadcast.92), dimensions={1}, to_apply=%all_to_all.220.reduce_sub_computation | reduce | bytes 2097156 | tf_op jit(solution)/shard_map/all_to_all | solution.py:96
  225.0 3.4 reshape.57
  228.3 3.7 copy.147
  232.1 3.6 fusion.82
  235.8 7.3 %fusion.3 = (f32[256,64,32]{0,1,2:T(8,128)S(1)}, f32[256,64,32]{0,1,2:T(8,128)S(1)}, f32[256,64,32]{0,1,2:T(8,128)}, f32[256,64,32]{0,1,2:T(8,128)}) fusion(f32[512,64,32]{0,1,2:T(8,128)S(1)} %fusion.82, f32[512,64,32]{0,1,2:T(8,128)} %fusion.83, f32[256,64,32]{0,2,1:T(8,128)S(1)} %bitcast.190, f32[512,64,32]{0,1,2:T(8,128)} %fusion.79, ...), kind=kLoop, calls=%fused_computation.7 | loop fusion | flops 4194304 | bytes 27262976 | tf_op jit(solution)/shard_map/mul | solution.py:105
  254.6 3.5 all-to-all-start.4
  258.1 3.0 copy.158
  263.6 9.0 %all-to-all-done.4 = f32[4,1,65536]{2,1,0:T(1,128)S(1)} async-done(((f32[4,1,65536]{2,1,0:T(1,128)}), f32[4,1,65536]{2,1,0:T(1,128)S(1)}, u32[]{:S(2)}, u32[]{:S(2)}) %all-to-all-start.4) | async-done | bytes 1048608 | tf_op jit(solution)/shard_map/all_to_all | solution.py:107
  272.5 4.5 all-to-all-start.5
  291.5 4.6 %all-to-all-start.12 = ((f32[4,1,65536]{2,1,0:T(1,128)}), f32[4,1,65536]{2,1,0:T(1,128)}, u32[]{:S(2)}, u32[]{:S(2)}) async-start(f32[4,1,65536]{2,1,0:T(1,128)} %reshape.44), calls=%async_computation.12 | async-start | bytes 2097152 | tf_op jit(solution)/shard_map/all_to_all | solution.py:107
  300.4 4.6 %reduce.13 = f32[4,65536]{1,0:T(4,128)S(1)} reduce(f32[4,1,65536]{2,1,0:T(1,128)} %copy-done.9, f32[]{:T(128)} %broadcast.92), dimensions={1}, to_apply=%all_to_all.224.reduce_sub_computation | reduce | bytes 2097156 | tf_op jit(solution)/shard_map/all_to_all | solution.py:107
  308.7 3.4 all_to_all.227
  312.1 4.6 %reduce.12 = f32[4,65536]{1,0:T(4,128)S(1)} reduce(f32[4,1,65536]{2,1,0:T(1,128)} %all-to-all-done.5, f32[]{:T(128)} %broadcast.92), dimensions={1}, to_apply=%all_to_all.228.reduce_sub_computation | reduce | bytes 2097156 | tf_op jit(solution)/shard_map/all_to_all | solution.py:107
  322.9 3.5 all-to-all-start.13
  334.1 6.7 %all-to-all-done.13 = f32[4,1,65536]{2,1,0:T(1,128)S(1)} async-done(((f32[4,1,65536]{2,1,0:T(1,128)}), f32[4,1,65536]{2,1,0:T(1,128)S(1)}, u32[]{:S(2)}, u32[]{:S(2)}) %all-to-all-start.13) | async-done | bytes 1048608 | tf_op jit(solution)/shard_map/all_to_all | solution.py:107
  340.9 5.1 %all-to-all-start.6 = ((f32[4,1,32768]{2,1,0:T(1,128)}), f32[4,1,32768]{2,1,0:T(1,128)}, u32[]{:S(2)}, u32[]{:S(2)}) async-start(f32[4,1,32768]{2,1,0:T(1,128)} %reshape.62), calls=%async_computation.6 | async-start | bytes 1048576 | tf_op jit(solution)/shard_map/all_to_all | solution.py:112
  350.5 4.6 %reduce.9 = f32[4,65536]{1,0:T(4,128)S(1)} reduce(f32[4,1,65536]{2,1,0:T(1,128)} %all-to-all-done.12, f32[]{:T(128)} %broadcast.92), dimensions={1}, to_apply=%all_to_all.256.reduce_sub_computation | reduce | bytes 2097156 | tf_op jit(solution)/shard_map/all_to_all | solution.py:107
  358.8 3.7 all_to_all.259
  362.5 3.7 reduce.8
  372.4 5.1 %all-to-all-start.7 = ((f32[4,1,32768]{2,1,0:T(1,128)}), f32[4,1,32768]{2,1,0:T(1,128)S(1)}, u32[]{:S(2)}, u32[]{:S(2)}) async-start(f32[4,1,32768]{2,1,0:T(1,128)} %reshape.64), calls=%async_computation.7 | async-start | bytes 1048576 | tf_op jit(solution)/shard_map/all_to_all | solution.py:112
  384.0 7.2 %all-to-all-done.7 = f32[4,1,32768]{2,1,0:T(1,128)S(1)} async-done(((f32[4,1,32768]{2,1,0:T(1,128)}), f32[4,1,32768]{2,1,0:T(1,128)S(1)}, u32[]{:S(2)}, u32[]{:S(2)}) %all-to-all-start.7) | async-done | bytes 524320 | tf_op jit(solution)/shard_map/all_to_all | solution.py:112
  391.2 3.5 all-to-all-start.14
  399.2 9.5 %all-to-all-done.14 = f32[4,1,32768]{2,1,0:T(1,128)S(1)} async-done(((f32[4,1,32768]{2,1,0:T(1,128)}), f32[4,1,32768]{2,1,0:T(1,128)S(1)}, u32[]{:S(2)}, u32[]{:S(2)}) %all-to-all-start.14) | async-done | bytes 524320 | tf_op jit(solution)/shard_map/all_to_all | solution.py:112
  408.7 4.3 all-to-all-start.15
  413.0 3.0 reduce.14
  443.2 3.0 reduce.11
  (159 shorter events, 166.3 us)
Async XLA Ops:
  5.9 20.8 %all-to-all-start.9 = ((f32[4,1,32768]{2,1,0:T(1,128)}), f32[4,1,32768]{2,1,0:T(1,128)S(1)}, u32[]{:S(2)}, u32[]{:S(2)}) async-start(f32[4,1,32768]{2,1,0:T(1,128)} %reshape.34), calls=%async_computation.9 | async-start | bytes 1048576 | tf_op jit(solution)/shard_map/all_to_all | solution.py:90
  26.8 6.6 %copy-start.16 = (f32[4,1,32768]{2,1,0:T(1,128)}, f32[4,1,32768]{2,1,0:T(1,128)S(1)}, u32[]{:S(2)}) copy-start(f32[4,1,32768]{2,1,0:T(1,128)S(1)} %all-to-all-done.9) | copy-start | bytes 1572868
  26.8 17.5 %all-to-all-start.8 = ((f32[4,1,32768]{2,1,0:T(1,128)}), f32[4,1,32768]{2,1,0:T(1,128)S(1)}, u32[]{:S(2)}, u32[]{:S(2)}) async-start(f32[4,1,32768]{2,1,0:T(1,128)} %reshape.36), calls=%async_computation.8 | async-start | bytes 1048576 | tf_op jit(solution)/shard_map/all_to_all | solution.py:90
  36.3 12.4 %copy-start.27 = (f32[128,32,32]{0,2,1:T(8,128)S(1)}, f32[128,32,32]{0,2,1:T(8,128)}, u32[]{:S(2)}) copy-start(f32[128,32,32]{0,2,1:T(8,128)} %get-tuple-element.23) | copy-start | bytes 1572868
  44.3 0.8 copy-start.17
  45.1 26.9 %all-to-all-start.1 = ((f32[4,1,32768]{2,1,0:T(1,128)}), f32[4,1,32768]{2,1,0:T(1,128)S(1)}, u32[]{:S(2)}, u32[]{:S(2)}) async-start(f32[4,1,32768]{2,1,0:T(1,128)} %reshape.50), calls=%async_computation.1 | async-start | bytes 1048576 | tf_op jit(solution)/shard_map/all_to_all | solution.py:90
  60.2 3.1 copy-start.18
  69.3 7.7 %copy-start.23 = (f32[32,32,128]{2,1,0:T(8,128)S(1)}, f32[32,32,128]{2,1,0:T(8,128)}, u32[]{:S(2)}) copy-start(f32[32,32,128]{2,1,0:T(8,128)} %all_to_all.247) | copy-start | bytes 1572868
  71.9 8.7 %copy-start.12 = (f32[4,1,32768]{2,1,0:T(1,128)}, f32[4,1,32768]{2,1,0:T(1,128)S(1)}, u32[]{:S(2)}) copy-start(f32[4,1,32768]{2,1,0:T(1,128)S(1)} %all-to-all-done.1) | copy-start | bytes 1572868
  71.9 18.6 %all-to-all-start = ((f32[4,1,32768]{2,1,0:T(1,128)}), f32[4,1,32768]{2,1,0:T(1,128)S(1)}, u32[]{:S(2)}, u32[]{:S(2)}) async-start(f32[4,1,32768]{2,1,0:T(1,128)} %reshape.52), calls=%async_computation | async-start | bytes 1048576 | tf_op jit(solution)/shard_map/all_to_all | solution.py:90
  90.5 0.8 copy-start.19
  91.3 34.4 %all-to-all-start.11 = ((f32[4,1,65536]{2,1,0:T(1,128)}), f32[4,1,65536]{2,1,0:T(1,128)S(1)}, u32[]{:S(2)}, u32[]{:S(2)}) async-start(f32[4,1,65536]{2,1,0:T(1,128)} %reshape.40), calls=%async_computation.11 | async-start | bytes 2097152 | tf_op jit(solution)/shard_map/all_to_all | solution.py:96
  99.2 4.9 %copy-start.13 = (f32[4,1,32768]{2,1,0:T(1,128)S(1)}, f32[4,1,32768]{2,1,0:T(1,128)}, u32[]{:S(2)}) copy-start(f32[4,1,32768]{2,1,0:T(1,128)} %copy-done.12) | copy-start | bytes 1572868
  112.0 3.1 copy-start.20
  122.9 6.4 %copy-start.24 = (f32[32,32,128]{2,1,0:T(8,128)S(1)}, f32[32,32,128]{2,1,0:T(8,128)}, u32[]{:S(2)}) copy-start(f32[32,32,128]{2,1,0:T(8,128)} %all_to_all.215) | copy-start | bytes 1572868
  125.7 18.7 %all-to-all-start.10 = ((f32[4,1,65536]{2,1,0:T(1,128)}), f32[4,1,65536]{2,1,0:T(1,128)S(1)}, u32[]{:S(2)}, u32[]{:S(2)}) async-start(f32[4,1,65536]{2,1,0:T(1,128)} %reshape.38), calls=%async_computation.10 | async-start | bytes 2097152 | tf_op jit(solution)/shard_map/all_to_all | solution.py:96
  144.4 12.7 %copy-start.7 = (f32[4,1,65536]{2,1,0:T(1,128)}, f32[4,1,65536]{2,1,0:T(1,128)S(1)}, u32[]{:S(2)}) copy-start(f32[4,1,65536]{2,1,0:T(1,128)S(1)} %all-to-all-done.10) | copy-start | bytes 3145732
  144.4 32.5 %all-to-all-start.2 = ((f32[4,1,65536]{2,1,0:T(1,128)}), f32[4,1,65536]{2,1,0:T(1,128)}, u32[]{:S(2)}, u32[]{:S(2)}) async-start(f32[4,1,65536]{2,1,0:T(1,128)} %reshape.54), calls=%async_computation.2 | async-start | bytes 2097152 | tf_op jit(solution)/shard_map/all_to_all | solution.py:96
  176.9 43.4 %all-to-all-start.3 = ((f32[4,1,65536]{2,1,0:T(1,128)}), f32[4,1,65536]{2,1,0:T(1,128)}, u32[]{:S(2)}, u32[]{:S(2)}) async-start(f32[4,1,65536]{2,1,0:T(1,128)} %reshape.56), calls=%async_computation.3 | async-start | bytes 2097152 | tf_op jit(solution)/shard_map/all_to_all | solution.py:96
  181.4 5.0 %copy-start.8 = (f32[4,1,65536]{2,1,0:T(1,128)S(1)}, f32[4,1,65536]{2,1,0:T(1,128)}, u32[]{:S(2)}) copy-start(f32[4,1,65536]{2,1,0:T(1,128)} %copy-done.7) | copy-start | bytes 3145732
  210.2 5.1 %copy-start.1 = (f32[4,64,32,32]{1,3,0,2:T(8,128)S(1)}, f32[4,64,32,32]{1,3,0,2:T(8,128)}, u32[]{:S(2)}) copy-start(f32[4,64,32,32]{1,3,0,2:T(8,128)} %copy.144) | copy-start | bytes 3145732
  232.1 3.7 copy-start
  232.1 3.7 copy-start.2
  254.6 17.9 %all-to-all-start.4 = ((f32[4,1,65536]{2,1,0:T(1,128)}), f32[4,1,65536]{2,1,0:T(1,128)S(1)}, u32[]{:S(2)}, u32[]{:S(2)}) async-start(f32[4,1,65536]{2,1,0:T(1,128)} %reshape.60), calls=%async_computation.4 | async-start | bytes 2097152 | tf_op jit(solution)/shard_map/all_to_all | solution.py:107
  263.6 13.4 %copy-start.4 = (f32[256,64,32]{0,1,2:T(8,128)S(1)}, f32[256,64,32]{0,1,2:T(8,128)}, u32[]{:S(2)}) copy-start(f32[256,64,32]{0,1,2:T(8,128)} %get-tuple-element.20) | copy-start | bytes 6291460
  272.5 7.5 %copy-start.9 = (f32[4,1,65536]{2,1,0:T(1,128)}, f32[4,1,65536]{2,1,0:T(1,128)S(1)}, u32[]{:S(2)}) copy-start(f32[4,1,65536]{2,1,0:T(1,128)S(1)} %all-to-all-done.4) | copy-start | bytes 3145732
  272.5 19.0 %all-to-all-start.5 = ((f32[4,1,65536]{2,1,0:T(1,128)}), f32[4,1,65536]{2,1,0:T(1,128)}, u32[]{:S(2)}, u32[]{:S(2)}) async-start(f32[4,1,65536]{2,1,0:T(1,128)} %reshape.58), calls=%async_computation.5 | async-start | bytes 2097152 | tf_op jit(solution)/shard_map/all_to_all | solution.py:107
  277.0 3.0 copy-start.3
  291.5 31.4 %all-to-all-start.12 = ((f32[4,1,65536]{2,1,0:T(1,128)}), f32[4,1,65536]{2,1,0:T(1,128)}, u32[]{:S(2)}, u32[]{:S(2)}) async-start(f32[4,1,65536]{2,1,0:T(1,128)} %reshape.44), calls=%async_computation.12 | async-start | bytes 2097152 | tf_op jit(solution)/shard_map/all_to_all | solution.py:107
  320.4 6.1 %copy-start.5 = (f32[256,32,32]{0,2,1:T(8,128)S(1)}, f32[256,32,32]{0,2,1:T(8,128)}, u32[]{:S(2)}) copy-start(f32[256,32,32]{0,2,1:T(8,128)} %all_to_all.227) | copy-start | bytes 3145732
  322.9 17.9 %all-to-all-start.13 = ((f32[4,1,65536]{2,1,0:T(1,128)}), f32[4,1,65536]{2,1,0:T(1,128)S(1)}, u32[]{:S(2)}, u32[]{:S(2)}) async-start(f32[4,1,65536]{2,1,0:T(1,128)} %reshape.42), calls=%async_computation.13 | async-start | bytes 2097152 | tf_op jit(solution)/shard_map/all_to_all | solution.py:107
  340.9 8.0 %copy-start.10 = (f32[4,1,65536]{2,1,0:T(1,128)}, f32[4,1,65536]{2,1,0:T(1,128)S(1)}, u32[]{:S(2)}) copy-start(f32[4,1,65536]{2,1,0:T(1,128)S(1)} %all-to-all-done.13) | copy-start | bytes 3145732
  340.9 31.5 %all-to-all-start.6 = ((f32[4,1,32768]{2,1,0:T(1,128)}), f32[4,1,32768]{2,1,0:T(1,128)}, u32[]{:S(2)}, u32[]{:S(2)}) async-start(f32[4,1,32768]{2,1,0:T(1,128)} %reshape.62), calls=%async_computation.6 | async-start | bytes 1048576 | tf_op jit(solution)/shard_map/all_to_all | solution.py:112
  358.8 3.7 copy-start.11
  369.8 7.7 %copy-start.6 = (f32[256,32,32]{0,2,1:T(8,128)S(1)}, f32[256,32,32]{0,2,1:T(8,128)}, u32[]{:S(2)}) copy-start(f32[256,32,32]{0,2,1:T(8,128)} %all_to_all.259) | copy-start | bytes 3145732
  372.4 18.7 %all-to-all-start.7 = ((f32[4,1,32768]{2,1,0:T(1,128)}), f32[4,1,32768]{2,1,0:T(1,128)S(1)}, u32[]{:S(2)}, u32[]{:S(2)}) async-start(f32[4,1,32768]{2,1,0:T(1,128)} %reshape.64), calls=%async_computation.7 | async-start | bytes 1048576 | tf_op jit(solution)/shard_map/all_to_all | solution.py:112
  391.2 8.0 %copy-start.14 = (f32[4,1,32768]{2,1,0:T(1,128)}, f32[4,1,32768]{2,1,0:T(1,128)S(1)}, u32[]{:S(2)}) copy-start(f32[4,1,32768]{2,1,0:T(1,128)S(1)} %all-to-all-done.7) | copy-start | bytes 1572868
  391.2 17.5 %all-to-all-start.14 = ((f32[4,1,32768]{2,1,0:T(1,128)}), f32[4,1,32768]{2,1,0:T(1,128)S(1)}, u32[]{:S(2)}, u32[]{:S(2)}) async-start(f32[4,1,32768]{2,1,0:T(1,128)} %reshape.46), calls=%async_computation.14 | async-start | bytes 1048576 | tf_op jit(solution)/shard_map/all_to_all | solution.py:112
  408.7 8.1 %copy-start.21 = (f32[4,1,32768]{2,1,0:T(1,128)}, f32[4,1,32768]{2,1,0:T(1,128)S(1)}, u32[]{:S(2)}) copy-start(f32[4,1,32768]{2,1,0:T(1,128)S(1)} %all-to-all-done.14) | copy-start | bytes 1572868
  408.7 34.6 %all-to-all-start.15 = ((f32[4,1,32768]{2,1,0:T(1,128)}), f32[4,1,32768]{2,1,0:T(1,128)}, u32[]{:S(2)}, u32[]{:S(2)}) async-start(f32[4,1,32768]{2,1,0:T(1,128)} %reshape.48), calls=%async_computation.15 | async-start | bytes 1048576 | tf_op jit(solution)/shard_map/all_to_all | solution.py:112
  419.5 2.5 copy-start.15
  427.5 2.5 copy-start.22
  449.7 2.5 copy-start.26
  449.7 3.4 copy-start.25
where the time goes:
time: 464 us; the launch traced here: 455 us
  local copies, waits for them, and re-layouts  205 us (44%)
  other arithmetic  73.7 us (16%)
  starting transfers between devices  68.6 us (15%)
  matrix products  54.7 us (12%)
  waiting for transfers between devices  51.8 us (11%)
    unnamed x90, local copies, waits for them, and re-layouts  71.3 us
    dot_general x10, matrix products, along_last(): jnp.einsum('kl,abl->kab', table, values, precision=lax.Precision.HIGHEST,...  30.1 us
    all_to_all x9, local copies, waits for them, and re-layouts, body(): lax.all_to_all(tuple(parts), 'py', split_axis=0, concat_axis=2, tiled=True)  24.7 us
    all_to_all x8, local copies, waits for them, and re-layouts, body(): lax.all_to_all(tuple(parts), 'px', split_axis=2, concat_axis=0, tiled=True)  23 us
    all_to_all x8, local copies, waits for them, and re-layouts, body(): lax.all_to_all(tuple(parts), 'py', split_axis=2, concat_axis=0, tiled=True)  20.9 us
    dot_general x12, matrix products, along_first(): jnp.einsum('kab,kl->abl', values, table, precision=lax.Precision.HIGHEST,...  20.6 us
    all_to_all x4, starting transfers between devices, body(): lax.all_to_all(tuple(parts), 'py', split_axis=0, concat_axis=2, tiled=True)  18.5 us
    all_to_all x4, starting transfers between devices, body(): lax.all_to_all(tuple(parts), 'py', split_axis=2, concat_axis=0, tiled=True)  18 us
  transfers between devices with their start and end apart: 16, of which 8 were waited for; matrix products, arithmetic and copies ran while one was open for 55% of the time, Pallas kernels for 0%

commit v1 on v0

v1 whole, which is shorter than its diff:
```python
import math

import jax
import jax.numpy as jnp
import numpy as np
from jax import lax
from jax.sharding import PartitionSpec as P

HIGH = lax.Precision.HIGH


def spectral_table(length, chunks):
    freq = np.arange(length).reshape(chunks, 1, length // chunks, 1)
    angle = (freq * np.arange(length) % (2 * length)) * (math.pi / length)
    both = np.concatenate([np.cos(angle), np.sin(angle)], 1)
    return both.reshape(2 * length, length).astype(np.float32)


def dot(spec, left, right):
    return jnp.einsum(spec, left, right, precision=HIGH, preferred_element_type=jnp.float32)


def kernel_block(factors, y_start, y_count, z_start, z_count):
    length = factors.shape[2] // 2
    weights = np.full((length,), 1.0 / length, np.float32)
    weights[0] = 0.5 / length
    factors = factors[:, :, :length] * weights
    factor_y = lax.dynamic_slice_in_dim(factors[1], y_start, y_count, 1)
    factor_z = lax.dynamic_slice_in_dim(factors[2], z_start, z_count, 1)
    pair = factor_z[:, :, None] * factor_y[:, None, :]
    return jnp.einsum("gzy,gx->zyx", pair, factors[0], precision=lax.Precision.HIGHEST)


def body(density, kernel_factors):
    replicas, rows_x, rows_y, length = density.shape
    count_px = lax.axis_size("px")
    count_py = lax.axis_size("py")
    half = count_px // replicas
    trade = [[i + half * r for r in range(replicas)] for i in range(half)]
    lines = [[r * half + i for i in range(half)] for r in range(replicas)]
    index_x = lax.axis_index("px") % half
    index_y = lax.axis_index("py")
    table_z = spectral_table(length, count_py)
    table_y = spectral_table(length, half)
    order = np.arange(length).reshape(replicas, half, rows_x).transpose(1, 0, 2).reshape(-1)
    table_x = spectral_table(length, 1)[:, order]

    held = lax.all_to_all(density, "px", 0, 0, axis_index_groups=trade, tiled=True)
    held = held.reshape(replicas * rows_x, rows_y, length)
    held = dot("kz,xyz->kyx", table_z, held)
    held = lax.all_to_all(held, "py", 0, 1, tiled=True)
    held = dot("qy,kyx->kqx", table_y, held)
    held = lax.all_to_all(held, "px", 1, 2, axis_index_groups=lines, tiled=True)
    z_freq, y_freq = length // count_py, length // half
    kernel = kernel_block(kernel_factors, index_x * y_freq, y_freq, index_y * z_freq, z_freq)
    held = dot("kqx,px->kqp", held, table_x)
    held = held.reshape(2, z_freq, 2, y_freq, 2, length) * kernel[None, :, None, :, None, :]
    held = held.reshape(2 * z_freq, 2 * y_freq, 2 * length)
    held = dot("kqp,px->kqx", held, table_x)
    held = lax.all_to_all(held, "px", 2, 1, axis_index_groups=lines, tiled=True)
    held = dot("kqx,qy->kyx", held, table_y)
    held = lax.all_to_all(held, "py", 1, 0, tiled=True)
    held = dot("kyx,kz->xyz", held, table_z)
    held = held.reshape(replicas, rows_x, rows_y, length)
    return lax.all_to_all(held, "px", 0, 0, axis_index_groups=trade, tiled=True)


def solution(mesh):
    placed = (P("rep", "px", "py", None), P())
    return jax.shard_map(
        body, mesh=mesh, in_specs=placed, out_specs=P("rep", "px", "py", None), check_vma=False
    )
```

time: 464 us -> 365 us (0.79)
  blocking collectives: 0 us -> 111 us
  local copies, waits for them, and re-layouts: 205 us -> 128 us
  starting transfers between devices: 68.6 us -> 5.28 us
  other arithmetic: 73.7 us -> 31.9 us
  matrix products: 54.7 us -> 37.4 us
  waiting for transfers between devices: 51.8 us -> 45.8 us
    all_to_all x0 -> x5, blocking collectives: none -> 111 us  [the longest x1 52 us: body(): held = lax.all_to_all(held, 'py', 1, 0, tiled=True)]
    all_to_all x16 -> x1, starting transfers between devices: 68.6 us -> 5.28 us  [body(): held = lax.all_to_all(held, 'py', 0, 1, tiled=True)]
    all_to_all x29 -> x6, local copies, waits for them, and re-layouts: 84.4 us -> 29.4 us  [the longest x1 15.3 us: body(): held = lax.all_to_all(held, 'px', 1, 2, axis_index_groups=lines, tiled=True)]
    unnamed x90 -> x25, local copies, waits for them, and re-layouts: 71.3 us -> 38.9 us
    all_to_all x16 -> x3, other arithmetic: 56 us -> 31.9 us  [the longest x1 16.5 us: body(): held = lax.all_to_all(held, 'px', 1, 2, axis_index_groups=lines, tiled=True)]
    dot_general x0 -> x3, local copies, waits for them, and re-layouts: none -> 21.4 us  [dot(): jnp.einsum(spec, left, right, precision=HIGH, preferred_element_type=jnp....]
    add x6 -> x0, local copies, waits for them, and re-layouts: 20.3 us -> none  [the longest x4 10.6 us: inverse_pair(): from_real[..., length:] + from_imag[..., :length]]
    sub x6 -> x0, local copies, waits for them, and re-layouts: 18.3 us -> none  [the longest x4 9.56 us: inverse_pair(): from_real[..., :length] - from_imag[..., length:]]
  transfers between devices with their start and end apart: 16 -> 1, of which waited for: 8 -> 1; matrix products, arithmetic and copies ran while one was open for 55% -> 0% of each run, Pallas kernels for 0% -> 0%
where the time goes in v1:
time: 365 us; the launch traced here: 360 us
  local copies, waits for them, and re-layouts  128 us (35%)
  blocking collectives  111 us (30%)
  waiting for transfers between devices  45.8 us (13%)
  matrix products  37.4 us (10%)
  other arithmetic  31.9 us (9%)
  starting transfers between devices  5.28 us (1%)
    all_to_all x1, blocking collectives, body(): held = lax.all_to_all(held, 'py', 1, 0, tiled=True)  52 us
    all_to_all x1, waiting for transfers between devices, body(): held = lax.all_to_all(held, 'py', 0, 1, tiled=True)  45.8 us
    unnamed x25, local copies, waits for them, and re-layouts  38.9 us
    dot_general x6, matrix products, dot(): jnp.einsum(spec, left, right, precision=HIGH, preferred_element_type=jnp....  36.5 us
    dot_general x3, local copies, waits for them, and re-layouts, dot(): jnp.einsum(spec, left, right, precision=HIGH, preferred_element_type=jnp....  21.4 us
    all_to_all x1, blocking collectives, body(): lax.all_to_all(density, 'px', 0, 0, axis_index_groups=trade, tiled=True)  18.8 us
    transpose x3, local copies, waits for them, and re-layouts, dot(): jnp.einsum(spec, left, right, precision=HIGH, preferred_element_type=jnp....  18.1 us
    all_to_all x1, other arithmetic, body(): held = lax.all_to_all(held, 'px', 1, 2, axis_index_groups=lines, tiled=True)  16.5 us
  transfers between devices with their start and end apart: 1, of which 1 were waited for; matrix products, arithmetic and copies ran while one was open for 0% of the time, Pallas kernels for 0%

profile of v1, /device:TPU:0, one launch (start us, length us, event | category | flops | bytes accessed | tf_op | source)
XLA Modules:
  0.0 359.6 jit_solution(2208279922184418932)
XLA Ops:
  0.0 0.0 copy-start.4
  0.0 18.8 %all_to_all.79 = f32[2,32,32,128]{3,2,1,0:T(8,128)S(1)} all-to-all(f32[2,32,32,128]{3,2,1,0:T(8,128)} %param.9), channel_id=1, replica_groups={{0,8},{4,12},{1,9},{5,13},{2,10},{6,14},{3,11},{7,15},{16,24},{20,28},{..., dimensions={0} | all-to-all | bytes 2097152 | tf_op jit(solution)/shard_map/all_to_all | solution.py:48
  18.8 0.6 copy.26
  19.4 0.0 copy-done.4
  19.4 1.0 convolution_bitcast_fusion.2
  20.4 4.5 %copy.27 = f32[256,32,64]{2,1,0:T(8,128)} copy(f32[256,32,64]{0,2,1:T(8,128)S(1)} %convolution_bitcast_fusion.2) | data formatting | bytes 4194304 | tf_op jit(solution)/shard_map/kz,xyz->kyx/transpose | solution.py:20
  24.9 0.0 copy-start.7
  24.9 0.0 copy-start.8
  24.9 5.5 %reshape.41 = f32[4,1,131072]{2,1,0:T(1,128)} reshape(f32[256,32,64]{2,1,0:T(8,128)} %copy.27) | data formatting | bytes 4194304
  30.4 5.3 %all-to-all-start.1 = ((f32[4,1,131072]{2,1,0:T(1,128)}), f32[4,1,131072]{2,1,0:T(1,128)S(1)}, u32[]{:S(2)}, u32[]{:S(2)}) async-start(f32[4,1,131072]{2,1,0:T(1,128)} %reshape.41), calls=%async_computation.1 | async-start | bytes 4194304 | tf_op jit(solution)/shard_map/all_to_all | solution.py:51
  35.7 0.0 copy-done.7
  35.8 0.0 copy-done.8
  35.8 0.1 constant_dynamic-slice_fusion.1
  35.9 0.1 copy.32
  36.0 0.1 constant_dynamic-slice_fusion
  36.0 0.1 copy.33
  36.1 1.0 fusion.6
  37.1 45.8 %all-to-all-done.1 = f32[4,1,131072]{2,1,0:T(1,128)S(1)} async-done(((f32[4,1,131072]{2,1,0:T(1,128)}), f32[4,1,131072]{2,1,0:T(1,128)S(1)}, u32[]{:S(2)}, u32[]{:S(2)}) %all-to-all-start.1) | async-done | bytes 2097184 | tf_op jit(solution)/shard_map/all_to_all | solution.py:51
  82.9 0.0 copy-start
  82.9 1.3 copy-done
  84.2 0.5 broadcast.3
  84.7 7.7 %reduce = f32[4,131072]{1,0:T(4,128)S(1)} reduce(f32[4,1,131072]{2,1,0:T(1,128)} %copy-done, f32[]{:T(128)} %broadcast.3), dimensions={1}, to_apply=%all_to_all.57.reduce_sub_computation | reduce | bytes 4194308 | tf_op jit(solution)/shard_map/all_to_all | solution.py:51
  92.4 3.9 %reshape.42 = f32[256,32,64]{2,1,0:T(8,128)} reshape(f32[4,131072]{1,0:T(4,128)S(1)} %reduce) | data formatting | bytes 4194304
  96.4 0.0 copy-start.3
  96.4 2.9 copy.28
  99.2 0.0 copy-done.3
  99.2 5.9 %convolution_bitcast_fusion = f32[64,256,64]{1,2,0:T(8,128)} fusion(f32[64,128,64]{2,1,0:T(8,128)S(1)} %bitcast.56, f32[256,128,1]{1,0,2:T(8,128)S(1)} %copy-done.3), kind=kOutput, calls=%fused_computation.6 | convolution fusion | flops 805306368 | bytes 6422528 | tf_op jit(solution)/shard_map/qy,kyx->kqx/dot_general | solution.py:20
  105.1 9.2 %copy.30 = f32[64,256,64]{2,0,1:T(8,128)} copy(f32[64,256,64]{1,2,0:T(8,128)} %convolution_bitcast_fusion) | data formatting | bytes 8388608 | tf_op jit(solution)/shard_map/qy,kyx->kqx/transpose | solution.py:20
  114.3 8.7 %reshape.43 = f32[2,1,524288]{2,1,0:T(1,128)} reshape(f32[256,64,64]{2,1,0:T(8,128)} %bitcast.52) | data formatting | bytes 8388608
  123.0 11.9 %all_to_all.80 = f32[2,1,524288]{2,1,0:T(1,128)} all-to-all(f32[2,1,524288]{2,1,0:T(1,128)} %reshape.43), channel_id=1, replica_groups={{0,4},{8,12},{1,5},{9,13},{2,6},{10,14},{3,7},{11,15},{16,20},{24,28},{..., dimensions={0} | all-to-all | bytes 8388608 | tf_op jit(solution)/shard_map/all_to_all | solution.py:53
  134.8 16.5 %reduce.1 = f32[2,524288]{1,0:T(2,128)} reduce(f32[2,1,524288]{2,1,0:T(1,128)} %all_to_all.80, f32[]{:T(128)} %broadcast.3), dimensions={1}, to_apply=%all_to_all.61.reduce_sub_computation | reduce | bytes 8388612 | tf_op jit(solution)/shard_map/all_to_all | solution.py:53
  151.3 9.9 %reshape.44 = f32[256,64,64]{2,1,0:T(8,128)} reshape(f32[2,524288]{1,0:T(2,128)} %reduce.1) | data formatting | bytes 8388608
  161.3 15.3 %copy.49 = f32[64,2,128,64]{3,1,2,0:T(2,128)} copy(f32[64,2,128,64]{3,0,2,1:T(8,128)} %bitcast.53) | data formatting | bytes 8388608 | tf_op jit(solution)/shard_map/all_to_all | solution.py:53
  176.6 0.0 copy-start.2
  176.6 9.0 %reshape.34 = f32[2,32,2,64,128,1]{4,3,2,1,0,5:T(8,128)} reshape(f32[64,128,2,64]{3,2,1,0:T(2,128)} %bitcast.54) | data formatting | bytes 8388608 | tf_op jit(solution)/shard_map/kqx,px->kqp/dot_general | solution.py:20
  185.6 0.0 copy-done.2
  185.6 5.6 %broadcast_multiply_fusion = f32[2,32,2,64,2,128]{5,3,4,2,1,0:T(8,128)S(1)} fusion(f32[32,64,128]{2,1,0:T(8,128)S(1)} %fusion.6, f32[2,128,128,1,1,1]{2,1,0,5,4,3:T(8,128)S(1)} %copy-done.2, f32[2,32,2,64,128,1]{4,3,2,1,0,5:T(8,128)} %reshape.34), kind=kOutput, calls=%fused_computation.5 | convolution fusion | flops 1612709888 | bytes 13762560 | tf_op jit(solution)/shard_map/kqx,px->kqp/dot_general | solution.py:20
  191.1 7.7 %copy.34 = f32[2,32,2,64,2,128]{5,4,3,2,1,0:T(2,128)} copy(f32[2,32,2,64,2,128]{5,3,4,2,1,0:T(8,128)S(1)} %broadcast_multiply_fusion) | data formatting | bytes 16777216 | tf_op jit(solution)/shard_map/mul | solution.py:57
  198.9 0.0 copy-start.1
  198.9 11.5 %reshape.22 = f32[64,128,256]{2,1,0:T(8,128)} reshape(f32[2,32,2,64,2,128]{5,4,3,2,1,0:T(2,128)} %copy.34) | data formatting | bytes 16777216 | tf_op jit(solution)/shard_map/reshape | solution.py:58
  210.4 0.0 copy-done.1
  210.4 8.8 %fusion.11 = f32[64,128,128]{2,1,0:T(8,128)} fusion(f32[64,128,256]{2,1,0:T(8,128)} %reshape.22, f32[256,128,1]{1,0,2:T(8,128)S(1)} %copy-done.1), kind=kOutput, calls=%fused_computation.18 | convolution fusion | flops 1610612736 | bytes 12713984 | tf_op jit(solution)/shard_map/kqp,px->kqx/dot_general | solution.py:20
  219.2 5.4 %copy.35 = f32[64,128,128]{1,0,2:T(8,128)} copy(f32[64,128,128]{2,1,0:T(8,128)} %fusion.11) | data formatting | bytes 8388608 | tf_op jit(solution)/shard_map/kqp,px->kqx/dot_general | solution.py:20
  224.6 12.1 %all_to_all.81 = f32[64,128,128]{1,0,2:T(8,128)} all-to-all(f32[64,128,128]{1,0,2:T(8,128)} %copy.35), channel_id=1, replica_groups={{0,4},{8,12},{1,5},{9,13},{2,6},{10,14},{3,7},{11,15},{16,20},{24,28},{..., dimensions={2} | all-to-all | bytes 8388608 | tf_op jit(solution)/shard_map/all_to_all | solution.py:60
  236.7 5.4 %copy.36 = f32[64,128,128]{2,1,0:T(8,128)} copy(f32[64,128,128]{1,0,2:T(8,128)} %all_to_all.81) | data formatting | bytes 8388608 | tf_op jit(solution)/shard_map/all_to_all | solution.py:60
  242.1 0.0 copy-start.6
  242.1 7.0 %reshape.24 = f32[64,256,64]{2,1,0:T(8,128)} reshape(f32[64,128,128]{2,1,0:T(8,128)} %copy.36) | data formatting | bytes 8388608 | tf_op jit(solution)/shard_map/kqx,qy->kyx/dot_general | solution.py:20
  249.1 0.0 copy-done.6
  249.1 10.0 %convolution_bitcast_fusion.1 = f32[64,128,64]{1,2,0:T(8,128)S(1)} fusion(f32[64,256,64]{2,1,0:T(8,128)} %reshape.24, f32[256,128,1]{1,0,2:T(8,128)S(1)} %copy-done.6), kind=kOutput, calls=%fused_computation.7 | convolution fusion | flops 805306368 | bytes 6422528 | tf_op jit(solution)/shard_map/kqx,qy->kyx/dot_general | solution.py:20
  259.1 4.5 %copy.38 = f32[64,128,64]{2,0,1:T(8,128)} copy(f32[64,128,64]{1,2,0:T(8,128)S(1)} %convolution_bitcast_fusion.1) | data formatting | bytes 4194304 | tf_op jit(solution)/shard_map/kqx,qy->kyx/transpose | solution.py:20
  263.6 4.5 %reshape.45 = f32[4,1,131072]{2,1,0:T(1,128)S(1)} reshape(f32[128,64,64]{2,1,0:T(8,128)} %bitcast.55) | data formatting | bytes 4194304
  268.1 52.0 %all_to_all.82 = f32[4,1,131072]{2,1,0:T(1,128)} all-to-all(f32[4,1,131072]{2,1,0:T(1,128)S(1)} %reshape.45), channel_id=1, replica_groups=mesh['rep'=2,'px'=4,'py'=4] {'py'}, dimensions={0} | all-to-all | bytes 4194304 | tf_op jit(solution)/shard_map/all_to_all | solution.py:62
  320.1 7.7 %reduce.2 = f32[4,131072]{1,0:T(4,128)S(1)} reduce(f32[4,1,131072]{2,1,0:T(1,128)} %all_to_all.82, f32[]{:T(128)} %broadcast.3), dimensions={1}, to_apply=%all_to_all.68.reduce_sub_computation | reduce | bytes 4194308 | tf_op jit(solution)/shard_map/all_to_all | solution.py:62
  327.9 3.9 %reshape.46 = f32[128,64,64]{2,1,0:T(8,128)} reshape(f32[4,131072]{1,0:T(4,128)S(1)} %reduce.2) | data formatting | bytes 4194304
  331.8 0.0 copy-start.5
  331.8 4.7 %copy.39 = f32[64,128,64]{2,1,0:T(8,128)S(1)} copy(f32[64,128,64]{2,0,1:T(8,128)} %bitcast.59) | data formatting | bytes 4194304 | tf_op jit(solution)/shard_map/all_to_all | solution.py:62
  336.5 0.0 copy-done.5
  336.5 5.2 %fusion.2 = f32[32,64,128]{2,1,0:T(8,128)S(1)} fusion(f32[256,128,1]{1,0,2:T(8,128)S(1)} %copy-done.5, f32[256,32,64]{2,1,0:T(8,128)S(1)} %bitcast.57), kind=kOutput, calls=%fused_computation.3 | convolution fusion | flops 402653184 | bytes 3276800 | tf_op jit(solution)/shard_map/kyx,kz->xyz/dot_general | solution.py:20
  341.7 0.6 copy.41
  342.3 15.8 %all_to_all.83 = f32[2,32,32,128]{3,2,1,0:T(8,128)S(1)} all-to-all(f32[2,32,32,128]{3,2,1,0:T(8,128)S(1)} %copy.41), channel_id=1, replica_groups={{0,8},{4,12},{1,9},{5,13},{2,10},{6,14},{3,11},{7,15},{16,24},{20,28},{..., dimensions={0} | all-to-all | bytes 2097152 | tf_op jit(solution)/shard_map/all_to_all | solution.py:65
  358.1 1.0 copy.51
  (2 shorter events, 0.0 us)
Async XLA Ops:
  0.0 19.4 %copy-start.4 = (f32[256,128,1]{1,0,2:T(8,128)S(1)}, f32[256,128,1]{1,0,2:T(8,128)}, u32[]{:S(2)}) copy-start(f32[256,128,1]{1,0,2:T(8,128)} %constant.48) | copy-start | bytes 393220
  24.9 10.8 %copy-start.7 = (f32[3,89,256]{2,1,0:T(8,128)S(1)}, f32[3,89,256]{2,1,0:T(8,128)}, u32[]{:S(2)}) copy-start(f32[3,89,256]{2,1,0:T(8,128)} %param.10) | copy-start | bytes 820228
  24.9 10.8 %copy-start.8 = (f32[128]{0:T(128)S(1)}, f32[128]{0:T(128)}, u32[]{:S(2)}) copy-start(f32[128]{0:T(128)} %constant.39.clone) | copy-start | bytes 1540
  30.4 52.4 %all-to-all-start.1 = ((f32[4,1,131072]{2,1,0:T(1,128)}), f32[4,1,131072]{2,1,0:T(1,128)S(1)}, u32[]{:S(2)}, u32[]{:S(2)}) async-start(f32[4,1,131072]{2,1,0:T(1,128)} %reshape.41), calls=%async_computation.1 | async-start | bytes 4194304 | tf_op jit(solution)/shard_map/all_to_all | solution.py:51
  82.9 1.3 copy-start
  96.4 2.9 copy-start.3
  176.6 9.0 %copy-start.2 = (f32[2,128,128,1,1,1]{2,1,0,5,4,3:T(8,128)S(1)}, f32[2,128,128,1,1,1]{2,1,0,5,4,3:T(8,128)}, u32[]{:S(2)}) copy-start(f32[2,128,128,1,1,1]{2,1,0,5,4,3:T(8,128)} %constant.50) | copy-start | bytes 393220
  198.9 11.5 %copy-start.1 = (f32[256,128,1]{1,0,2:T(8,128)S(1)}, f32[256,128,1]{1,0,2:T(8,128)}, u32[]{:S(2)}) copy-start(f32[256,128,1]{1,0,2:T(8,128)} %constant.51) | copy-start | bytes 393220
  242.1 7.0 %copy-start.6 = (f32[256,128,1]{1,0,2:T(8,128)S(1)}, f32[256,128,1]{1,0,2:T(8,128)}, u32[]{:S(2)}) copy-start(f32[256,128,1]{1,0,2:T(8,128)} %constant.52) | copy-start | bytes 393220
  331.8 4.7 %copy-start.5 = (f32[256,128,1]{1,0,2:T(8,128)S(1)}, f32[256,128,1]{1,0,2:T(8,128)}, u32[]{:S(2)}) copy-start(f32[256,128,1]{1,0,2:T(8,128)} %constant.53) | copy-start | bytes 393220

commit v2 on v1

--- a/solution.py
+++ b/solution.py
@@ -4,9 +4,12 @@
 import jax.numpy as jnp
 import numpy as np
 from jax import lax
+from jax.experimental import pallas as pl
+from jax.experimental.pallas import tpu as pltpu
 from jax.sharding import PartitionSpec as P
 
-HIGH = lax.Precision.HIGH
+HIGHEST = lax.Precision.HIGHEST
+BLOCK = 8
 
 
 def spectral_table(length, chunks):
@@ -17,7 +20,7 @@
 
 
 def dot(spec, left, right):
-    return jnp.einsum(spec, left, right, precision=HIGH, preferred_element_type=jnp.float32)
+    return jnp.einsum(spec, left, right, precision=HIGHEST, preferred_element_type=jnp.float32)
 
 
 def kernel_block(factors, y_start, y_count, z_start, z_count):
@@ -31,7 +34,7 @@
     return jnp.einsum("gzy,gx->zyx", pair, factors[0], precision=lax.Precision.HIGHEST)
 
 
-def body(density, kernel_factors):
+def plain_body(density, kernel_factors):
     replicas, rows_x, rows_y, length = density.shape
     count_px = lax.axis_size("px")
     count_py = lax.axis_size("py")
@@ -65,6 +68,254 @@
     return lax.all_to_all(held, "px", 0, 0, axis_index_groups=trade, tiled=True)
 
 
+def split(values, axis, third_low=False):
+    high = values.astype(jnp.bfloat16)
+    low = (values - high.astype(jnp.float32)).astype(jnp.bfloat16)
+    return jnp.concatenate([high, high, low] if third_low else [high, low, high], axis)
+
+
+def matmul(left, right, contract=((1,), (0,))):
+    return lax.dot_general(left, right, (contract, ((), ())), preferred_element_type=jnp.float32)
+
+
+def solve_kernel(
+    dens, factors, fwd_z, fwd_y, fwd_x, inv_x, inv_y, inv_z, out,
+    traded, a_send, a_held, b_send, b_held, g_send, g_held, h_send, h_held, o_send, o_held,
+    sems_t, sems_z, sems_x, sems_xi, sems_zi, sems_ti,
+):
+    replicas, rows_x, rows_y, length = dens.shape
+    count_py = lax.axis_size("py")
+    half = lax.axis_size("px") // replicas
+    me_px, me_py = lax.axis_index("px"), lax.axis_index("py")
+    mine, line = lax.div(me_px, half), lax.rem(me_px, half)
+    lanes = 2 * length // half
+    mid = lanes // 2
+    freq_z, freq_y = length // count_py, length // half
+    blocks_y, blocks_f = rows_y // BLOCK, freq_z // BLOCK
+    started = []
+
+    def send(src, dst, sems, slot, device):
+        copy = pltpu.make_async_remote_copy(
+            src_ref=src, dst_ref=dst, send_sem=sems.at[(0,) + slot], recv_sem=sems.at[(1,) + slot],
+            device_id=device, device_id_type=pl.DeviceIdType.MESH,
+        )
+        copy.start()
+        started.append(copy)
+        return copy
+
+    trades = []
+    for block in range(blocks_y):
+        rows = pl.ds(block * BLOCK, BLOCK)
+        for step in range(1, replicas):
+            other = lax.rem(mine + step, replicas)
+            trades.append(
+                send(dens.at[other, :, rows, :], traded.at[mine, :, rows, :], sems_t,
+                     (step, block), {"px": line + half * other})
+            )
+    traded[mine] = dens[mine]
+    traded_rows = traded.reshape(replicas * rows_x * rows_y, length)
+    a_rows = a_send.reshape(length * rows_y, lanes)
+
+    arrivals = []
+    for block in range(blocks_y):
+        for copy in trades[block * (replicas - 1) : (block + 1) * (replicas - 1)]:
+            copy.wait_recv()
+
+        @pl.loop(0, BLOCK)
+        def _(step, block=block):
+            y = block * BLOCK + step
+            cells = traded_rows[pl.ds(y, replicas * rows_x, stride=rows_y), :]
+            waves = matmul(fwd_z[...], split(cells, 1), ((1,), (1,)))
+            both = jnp.concatenate([waves[:length], waves[length:]], 1)
+            a_rows[pl.ds(y, length, stride=rows_y), :] = both
+
+        rows = pl.ds(block * BLOCK, BLOCK)
+        there = pl.ds(pl.multiple_of(me_py * rows_y + block * BLOCK, BLOCK), BLOCK)
+        for step in (2, 1, 3) if count_py == 4 else range(1, count_py):
+            other = lax.rem(me_py + step, count_py)
+            arrivals.append(
+                send(a_send.at[pl.ds(other * freq_z, freq_z), rows, :], a_held.at[:, there, :],
+                     sems_z, (step, block), {"py": other})
+            )
+        a_held[:, there, :] = a_send[pl.ds(me_py * freq_z, freq_z), rows, :]
+    for copy in arrivals:
+        copy.wait_recv()
+
+    arrivals = []
+    for block in range(blocks_f):
+
+        @pl.loop(block * BLOCK, (block + 1) * BLOCK)
+        def _(f):
+            waves = matmul(fwd_y[...], split(a_held[f], 0))
+            for part in range(half):
+                b_send[part, f] = waves[part * 2 * freq_y : (part + 1) * 2 * freq_y]
+            b_held[line, f] = b_send[line, f]
+
+        some = pl.ds(block * BLOCK, BLOCK)
+        here = []
+        for step in range(1, half):
+            other = lax.rem(line + step, half)
+            here.append(
+                send(b_send.at[other, some], b_held.at[line, some], sems_x, (step, block),
+                     {"px": mine * half + other})
+            )
+        arrivals.append(here)
+
+    factor_y = factors[1, pl.ds(pl.multiple_of(line * freq_y, BLOCK), freq_y), :]
+    returns, arrivals_z = [], []
+
+    def finish_lines(block):
+        for copy in returns[block]:
+            copy.wait_recv()
+
+        @pl.loop(block * BLOCK, (block + 1) * BLOCK)
+        def _(f):
+            waves = jnp.concatenate([g_held[part, f] for part in range(half)], 0)
+            h_send[f] = matmul(inv_y[...], split(waves, 0))
+            own = pl.ds(pl.multiple_of(me_py * rows_y, BLOCK), rows_y)
+            h_held[me_py * freq_z + f] = h_send[f, own, :]
+
+        some = pl.ds(block * BLOCK, BLOCK)
+        there = pl.ds(me_py * freq_z + block * BLOCK, BLOCK)
+        for step in (2, 1, 3) if count_py == 4 else range(1, count_py):
+            other = lax.rem(me_py + step, count_py)
+            cells = pl.ds(pl.multiple_of(other * rows_y, BLOCK), rows_y)
+            arrivals_z.append(
+                send(h_send.at[some, cells, :], h_held.at[there], sems_zi, (step, block),
+                     {"py": other})
+            )
+
+    for block in range(blocks_f):
+        for copy in arrivals[block]:
+            copy.wait_recv()
+
+        @pl.loop(block * BLOCK, (block + 1) * BLOCK)
+        def _(f):
+            row = factors[2, pl.ds(me_py * freq_z + f, 1), :]
+            kernel = lax.dot_general(
+                factor_y * row, factors[0], (((1,), (1,)), ((), ())),
+                precision=HIGHEST, preferred_element_type=jnp.float32,
+            )
+            kernel = jnp.concatenate([kernel, kernel], 1)
+            kernel = jnp.concatenate([kernel] * 4, 0)
+            ours = [b_held[part, f] for part in range(half)]
+            cosines = jnp.concatenate([value[:, :mid] for value in ours], 1)
+            sines = jnp.concatenate([value[:, mid:] for value in ours], 1)
+            cells = jnp.concatenate([cosines, sines], 0)
+            product = matmul(split(cells, 1), fwd_x[...]) * kernel
+            cells = matmul(split(product, 1), inv_x[...])
+            cosines, sines = cells[: 2 * freq_y], cells[2 * freq_y :]
+            for part in range(half):
+                cut = slice(part * mid, (part + 1) * mid)
+                g_send[part, f] = jnp.concatenate([cosines[:, cut], sines[:, cut]], 1)
+            g_held[line, f] = g_send[line, f]
+
+        some = pl.ds(block * BLOCK, BLOCK)
+        here = []
+        for step in range(1, half):
+            other = lax.rem(line + step, half)
+            here.append(
+                send(g_send.at[other, some], g_held.at[line, some], sems_xi, (step, block),
+                     {"px": mine * half + other})
+            )
+        returns.append(here)
+        if block:
+            finish_lines(block - 1)
+    finish_lines(blocks_f - 1)
+    for copy in arrivals_z:
+        copy.wait_recv()
+
+    h_rows = h_held.reshape(length * rows_y, lanes)
+    o_rows = o_send.reshape(replicas * rows_x * rows_y, length)
+    arrivals = []
+    for block in range(blocks_y):
+
+        @pl.loop(block * BLOCK, (block + 1) * BLOCK)
+        def _(y):
+            waves = h_rows[pl.ds(y, length, stride=rows_y), :].T
+            waves = jnp.concatenate([waves[:mid], waves[mid:]], 1)
+            cells = matmul(split(waves, 1), inv_z[...])
+            o_rows[pl.ds(y, replicas * rows_x, stride=rows_y), :] = cells
+
+        rows = pl.ds(block * BLOCK, BLOCK)
+        for step in range(1, replicas):
+            other = lax.rem(mine + step, replicas)
+            arrivals.append(
+                send(o_send.at[other, :, rows, :], o_held.at[mine, :, rows, :], sems_ti,
+                     (step, block), {"px": line + half * other})
+            )
+    out[mine] = o_send[mine]
+    for copy in arrivals:
+        copy.wait_recv()
+    for step in range(1, replicas):
+        other = lax.rem(mine + step, replicas)
+        out[other] = o_held[other]
+    for copy in started:
+        copy.wait_send()
+
+
+def kernel_body(density, kernel_factors):
+    replicas, rows_x, rows_y, length = density.shape
+    count_py = lax.axis_size("py")
+    half = lax.axis_size("px") // replicas
+    lanes = 2 * length // half
+    freq_z, freq_y = length // count_py, length // half
+    weights = np.full((length,), 1.0 / length, np.float32)
+    weights[0] = 0.5 / length
+    terms = kernel_factors.shape[1]
+    factors = (kernel_factors[:, :, :length] * weights).transpose(0, 2, 1)
+    factors = jnp.pad(factors, ((0, 0), (0, 0), (0, -terms % 128)))
+    order = np.arange(length).reshape(replicas, half, rows_x).transpose(1, 0, 2).reshape(-1)
+    table_z = spectral_table(length, 1)
+    table_y = spectral_table(length, half)
+    table_x = spectral_table(length, 1)[:, order]
+
+    def held(table, axis):
+        high = table.astype(jnp.bfloat16)
+        low = (table - high.astype(np.float32)).astype(jnp.bfloat16)
+        return jnp.asarray(np.concatenate([high, high, low], axis))
+
+    tables = (
+        held(table_z, 1), held(table_y, 1), held(table_x.T, 0),
+        held(table_x, 0), held(table_y.T, 1), held(table_z, 0),
+    )
+    f32 = jnp.float32
+    lines = (length, rows_y, lanes)
+    whole = (freq_z, length, lanes)
+    pairs = (half, freq_z, 2 * freq_y, lanes)
+    blocks_y, blocks_f = rows_y // BLOCK, freq_z // BLOCK
+    dma = pltpu.SemaphoreType.DMA
+    return pl.pallas_call(
+        solve_kernel,
+        out_shape=jax.ShapeDtypeStruct(density.shape, f32),
+        in_specs=[pl.BlockSpec(memory_space=pltpu.VMEM)] * 8,
+        out_specs=pl.BlockSpec(memory_space=pltpu.VMEM),
+        scratch_shapes=[
+            pltpu.VMEM(density.shape, f32),
+            pltpu.VMEM(lines, f32), pltpu.VMEM(whole, f32),
+            pltpu.VMEM(pairs, f32), pltpu.VMEM(pairs, f32),
+            pltpu.VMEM(pairs, f32), pltpu.VMEM(pairs, f32),
+            pltpu.VMEM(whole, f32), pltpu.VMEM(lines, f32),
+            pltpu.VMEM(density.shape, f32), pltpu.VMEM(density.shape, f32),
+            dma((2, replicas, blocks_y)), dma((2, count_py, blocks_y)),
+            dma((2, half, blocks_f)), dma((2, half, blocks_f)),
+            dma((2, count_py, blocks_f)), dma((2, replicas, blocks_y)),
+        ],
+        compiler_params=pltpu.CompilerParams(
+            has_side_effects=True, vmem_limit_bytes=56 * 2**20
+        ),
+    )(density, factors, *tables)
+
+
+def body(density, kernel_factors):
+    replicas, _, rows_y, length = density.shape
+    lanes = 2 * length * replicas // lax.axis_size("px")
+    freq_z = length // lax.axis_size("py")
+    if lanes % 128 == 0 and rows_y % BLOCK == 0 and freq_z % BLOCK == 0:
+        return kernel_body(density, kernel_factors)
+    return plain_body(density, kernel_factors)
+
+
 def solution(mesh):
     placed = (P("rep", "px", "py", None), P())
     return jax.shard_map(

time: 365 us -> 148 us (0.41); the launches traced: 360 us -> 148 us
  Pallas kernels: 0 us -> 143 us
  local copies, waits for them, and re-layouts: 128 us -> 4.51 us
  blocking collectives: 111 us -> 0 us
  waiting for transfers between devices: 45.8 us -> 0 us
  matrix products: 37.4 us -> 0 us
  other arithmetic: 31.9 us -> 0.08 us
  starting transfers between devices: 5.28 us -> 0 us
    pallas_call x0 -> x1, Pallas kernels: none -> 143 us  [kernel_body(): pl.pallas_call(solve_kernel, out_shape=jax.ShapeDtypeStruct(density.shape...]
    all_to_all x5 -> x0, blocking collectives: 111 us -> none  [the longest x1 52 us: body(): held = lax.all_to_all(held, 'py', 1, 0, tiled=True)]
    all_to_all x1 -> x0, waiting for transfers between devices: 45.8 us -> none  [body(): held = lax.all_to_all(held, 'py', 0, 1, tiled=True)]
    dot_general x7 -> x0, matrix products: 37.4 us -> none  [the longest x6 36.5 us: dot(): jnp.einsum(spec, left, right, precision=HIGH, preferred_element_type=jnp....]
    unnamed x25 -> x4, local copies, waits for them, and re-layouts: 38.9 us -> 2.91 us
    all_to_all x3 -> x0, other arithmetic: 31.9 us -> none  [the longest x1 16.5 us: body(): held = lax.all_to_all(held, 'px', 1, 2, axis_index_groups=lines, tiled=True)]
    all_to_all x6 -> x0, local copies, waits for them, and re-layouts: 29.4 us -> none  [the longest x1 15.3 us: body(): held = lax.all_to_all(held, 'px', 1, 2, axis_index_groups=lines, tiled=True)]
    dot_general x3 -> x0, local copies, waits for them, and re-layouts: 21.4 us -> none  [dot(): jnp.einsum(spec, left, right, precision=HIGH, preferred_element_type=jnp....]
  transfers between devices with their start and end apart: 1 -> 0, of which waited for: 1 -> 0; matrix products, arithmetic and copies ran while one was open for 0% -> 0% of each run, Pallas kernels for 0% -> 0%
where the time goes in v2:
time: 148 us
  Pallas kernels  143 us (97%)
  local copies, waits for them, and re-layouts  4.51 us (3%)
    pallas_call x1, Pallas kernels, kernel_body(): pl.pallas_call(solve_kernel, out_shape=jax.ShapeDtypeStruct(density.shape...  143 us

profile of v2, /device:TPU:0, one launch (start us, length us, event | category | flops | bytes accessed | tf_op | source)
XLA Modules:
  0.0 147.6 jit_solution(13302635310306872440)
XLA Ops:
  0.0 0.0 slice-start
  0.0 0.9 slice-done
  0.9 0.0 copy-start
  0.9 0.1 copy.11
  1.0 0.5 copy-done
  1.6 0.1 multiply_bitcast_fusion
  1.7 0.7 pad.4.factors
  2.4 143.0 %shard_map.91 = f32[2,32,32,128]{3,2,1,0:T(8,128)} custom-call(f32[2,32,32,128]{3,2,1,0:T(8,128)} %dens.1, f32[3,128,128]{2,1,0:T(8,128)} %pad.4.factors, bf16[256,384]{1,0:T(8,128)(2,1)} %constant.18.clone.fwd_z, bf16[256,384]{1,0:T(8,128)(2,1)} %constant.19.clone.fwd_y, bf16[384,256]{1,0:T(8,128)(2,1)} %constant.20.clone.fwd_x, ...), custom_call_target="tpu_custom_call" | custom-call | tf_op jit(solution)/shard_map/pallas_call | solution.py:288
  145.4 2.3 %copy.13 = f32[2,32,32,128]{3,2,1,0:T(8,128)} copy(f32[2,32,32,128]{3,2,1,0:T(8,128)} %shard_map.91) | data formatting | bytes 2097152
Async XLA Ops:
  0.0 0.9 slice-start
  0.9 0.7 copy-start

commit v3 on v2

--- a/solution.py
+++ b/solution.py
@@ -116,7 +116,21 @@
     traded_rows = traded.reshape(replicas * rows_x * rows_y, length)
     a_rows = a_send.reshape(length * rows_y, lanes)
 
-    arrivals = []
+    first = blocks_y // 2
+    peers = (2, 1, 3) if count_py == 4 else range(1, count_py)
+    arrivals_y = [[] for _ in range(blocks_f)]
+
+    def send_planes(freq, rows, there, slot):
+        for step in peers:
+            other = lax.rem(me_py + step, count_py)
+            theirs = pl.ds(other * freq_z + freq.start, freq.size)
+            arrivals_y[freq.start // BLOCK].append(
+                send(a_send.at[theirs, rows, :], a_held.at[freq, there, :], sems_z,
+                     (step, slot), {"py": other})
+            )
+        ours = pl.ds(me_py * freq_z + freq.start, freq.size)
+        a_held[freq, there, :] = a_send[ours, rows, :]
+
     for block in range(blocks_y):
         for copy in trades[block * (replicas - 1) : (block + 1) * (replicas - 1)]:
             copy.wait_recv()
@@ -129,20 +143,21 @@
             both = jnp.concatenate([waves[:length], waves[length:]], 1)
             a_rows[pl.ds(y, length, stride=rows_y), :] = both
 
-        rows = pl.ds(block * BLOCK, BLOCK)
-        there = pl.ds(pl.multiple_of(me_py * rows_y + block * BLOCK, BLOCK), BLOCK)
-        for step in (2, 1, 3) if count_py == 4 else range(1, count_py):
-            other = lax.rem(me_py + step, count_py)
-            arrivals.append(
-                send(a_send.at[pl.ds(other * freq_z, freq_z), rows, :], a_held.at[:, there, :],
-                     sems_z, (step, block), {"py": other})
-            )
-        a_held[:, there, :] = a_send[pl.ds(me_py * freq_z, freq_z), rows, :]
-    for copy in arrivals:
-        copy.wait_recv()
+        if block < first:
+            rows = pl.ds(block * BLOCK, BLOCK)
+            there = pl.ds(pl.multiple_of(me_py * rows_y + block * BLOCK, BLOCK), BLOCK)
+            send_planes(pl.ds(0, freq_z), rows, there, block)
+    count = rows_y - first * BLOCK
+    for block in range(blocks_f):
+        rows = pl.ds(first * BLOCK, count)
+        there = pl.ds(pl.multiple_of(me_py * rows_y + first * BLOCK, BLOCK), count)
+        send_planes(pl.ds(block * BLOCK, BLOCK), rows, there, first + block)
 
     arrivals = []
-    for block in range(blocks_f):
+
+    def start_lines(block):
+        for copy in arrivals_y[block]:
+            copy.wait_recv()
 
         @pl.loop(block * BLOCK, (block + 1) * BLOCK)
         def _(f):
@@ -162,7 +177,8 @@
         arrivals.append(here)
 
     factor_y = factors[1, pl.ds(pl.multiple_of(line * freq_y, BLOCK), freq_y), :]
-    returns, arrivals_z = [], []
+    returns = []
+    arrivals_z = [[] for _ in range(blocks_y)]
 
     def finish_lines(block):
         for copy in returns[block]:
@@ -177,15 +193,19 @@
 
         some = pl.ds(block * BLOCK, BLOCK)
         there = pl.ds(me_py * freq_z + block * BLOCK, BLOCK)
-        for step in (2, 1, 3) if count_py == 4 else range(1, count_py):
-            other = lax.rem(me_py + step, count_py)
-            cells = pl.ds(pl.multiple_of(other * rows_y, BLOCK), rows_y)
-            arrivals_z.append(
-                send(h_send.at[some, cells, :], h_held.at[there], sems_zi, (step, block),
-                     {"py": other})
-            )
-
-    for block in range(blocks_f):
+        last = block == blocks_f - 1
+        size = BLOCK if last else rows_y
+        for cut in range(rows_y // size):
+            for step in peers:
+                other = lax.rem(me_py + step, count_py)
+                cells = pl.ds(pl.multiple_of(other * rows_y + cut * size, BLOCK), size)
+                copy = send(
+                    h_send.at[some, cells, :], h_held.at[there, pl.ds(cut * size, size), :],
+                    sems_zi, (step, block + cut), {"py": other},
+                )
+                arrivals_z[cut].append(copy)
+
+    def solve_lines(block):
         for copy in arrivals[block]:
             copy.wait_recv()
 
@@ -219,16 +239,21 @@
                      {"px": mine * half + other})
             )
         returns.append(here)
-        if block:
-            finish_lines(block - 1)
-    finish_lines(blocks_f - 1)
-    for copy in arrivals_z:
-        copy.wait_recv()
+
+    for stage in range(blocks_f + 2):
+        if stage < blocks_f:
+            start_lines(stage)
+        if 0 <= stage - 1 < blocks_f:
+            solve_lines(stage - 1)
+        if 0 <= stage - 2:
+            finish_lines(stage - 2)
 
     h_rows = h_held.reshape(length * rows_y, lanes)
     o_rows = o_send.reshape(replicas * rows_x * rows_y, length)
     arrivals = []
     for block in range(blocks_y):
+        for copy in arrivals_z[block]:
+            copy.wait_recv()
 
         @pl.loop(block * BLOCK, (block + 1) * BLOCK)
         def _(y):
@@ -297,9 +322,9 @@
             pltpu.VMEM(pairs, f32), pltpu.VMEM(pairs, f32),
             pltpu.VMEM(whole, f32), pltpu.VMEM(lines, f32),
             pltpu.VMEM(density.shape, f32), pltpu.VMEM(density.shape, f32),
-            dma((2, replicas, blocks_y)), dma((2, count_py, blocks_y)),
+            dma((2, replicas, blocks_y)), dma((2, count_py, blocks_y // 2 + blocks_f)),
             dma((2, half, blocks_f)), dma((2, half, blocks_f)),
-            dma((2, count_py, blocks_f)), dma((2, replicas, blocks_y)),
+            dma((2, count_py, blocks_f + blocks_y)), dma((2, replicas, blocks_y)),
         ],
         compiler_params=pltpu.CompilerParams(
             has_side_effects=True, vmem_limit_bytes=56 * 2**20

time: 148 us -> 139 us (0.939)
  Pallas kernels: 143 us -> 134 us
    pallas_call x1, Pallas kernels: 143 us -> 134 us  [kernel_body(): pl.pallas_call(solve_kernel, out_shape=jax.ShapeDtypeStruct(density.shape...]
where the time goes in v3:
time: 139 us; the launch traced here: 138 us
  Pallas kernels  134 us (96%)
  local copies, waits for them, and re-layouts  4.51 us (3%)
    pallas_call x1, Pallas kernels, kernel_body(): pl.pallas_call(solve_kernel, out_shape=jax.ShapeDtypeStruct(density.shape...  134 us
    unnamed x4, local copies, waits for them, and re-layouts  2.91 us

profile of v3, /device:TPU:0, one launch (start us, length us, event | category | flops | bytes accessed | tf_op | source)
XLA Modules:
  0.0 138.4 jit_solution(14778221618002327725)
XLA Ops:
  0.0 0.0 slice-start
  0.0 0.9 slice-done
  0.9 0.0 copy-start
  0.9 0.1 copy.11
  1.0 0.5 copy-done
  1.6 0.1 multiply_bitcast_fusion
  1.7 0.7 pad.4.factors
  2.4 133.7 %shard_map.91 = f32[2,32,32,128]{3,2,1,0:T(8,128)} custom-call(f32[2,32,32,128]{3,2,1,0:T(8,128)} %dens.1, f32[3,128,128]{2,1,0:T(8,128)} %pad.4.factors, bf16[256,384]{1,0:T(8,128)(2,1)} %constant.18.clone.fwd_z, bf16[256,384]{1,0:T(8,128)(2,1)} %constant.19.clone.fwd_y, bf16[384,256]{1,0:T(8,128)(2,1)} %constant.20.clone.fwd_x, ...), custom_call_target="tpu_custom_call" | custom-call | tf_op jit(solution)/shard_map/pallas_call | solution.py:313
  136.1 2.3 %copy.13 = f32[2,32,32,128]{3,2,1,0:T(8,128)} copy(f32[2,32,32,128]{3,2,1,0:T(8,128)} %shard_map.91) | data formatting | bytes 2097152
Async XLA Ops:
  0.0 0.9 slice-start
  0.9 0.7 copy-start

commit v4 on v3

--- a/solution.py
+++ b/solution.py
@@ -116,7 +116,7 @@
     traded_rows = traded.reshape(replicas * rows_x * rows_y, length)
     a_rows = a_send.reshape(length * rows_y, lanes)
 
-    first = blocks_y // 2
+    first = blocks_y // 4
     peers = (2, 1, 3) if count_py == 4 else range(1, count_py)
     arrivals_y = [[] for _ in range(blocks_f)]
 
@@ -135,7 +135,7 @@
         for copy in trades[block * (replicas - 1) : (block + 1) * (replicas - 1)]:
             copy.wait_recv()
 
-        @pl.loop(0, BLOCK)
+        @pl.loop(0, BLOCK, unroll=4)
         def _(step, block=block):
             y = block * BLOCK + step
             cells = traded_rows[pl.ds(y, replicas * rows_x, stride=rows_y), :]
@@ -159,7 +159,7 @@
         for copy in arrivals_y[block]:
             copy.wait_recv()
 
-        @pl.loop(block * BLOCK, (block + 1) * BLOCK)
+        @pl.loop(block * BLOCK, (block + 1) * BLOCK, unroll=4)
         def _(f):
             waves = matmul(fwd_y[...], split(a_held[f], 0))
             for part in range(half):
@@ -184,7 +184,7 @@
         for copy in returns[block]:
             copy.wait_recv()
 
-        @pl.loop(block * BLOCK, (block + 1) * BLOCK)
+        @pl.loop(block * BLOCK, (block + 1) * BLOCK, unroll=4)
         def _(f):
             waves = jnp.concatenate([g_held[part, f] for part in range(half)], 0)
             h_send[f] = matmul(inv_y[...], split(waves, 0))
@@ -209,7 +209,7 @@
         for copy in arrivals[block]:
             copy.wait_recv()
 
-        @pl.loop(block * BLOCK, (block + 1) * BLOCK)
+        @pl.loop(block * BLOCK, (block + 1) * BLOCK, unroll=4)
         def _(f):
             row = factors[2, pl.ds(me_py * freq_z + f, 1), :]
             kernel = lax.dot_general(
@@ -255,7 +255,7 @@
         for copy in arrivals_z[block]:
             copy.wait_recv()
 
-        @pl.loop(block * BLOCK, (block + 1) * BLOCK)
+        @pl.loop(block * BLOCK, (block + 1) * BLOCK, unroll=4)
         def _(y):
             waves = h_rows[pl.ds(y, length, stride=rows_y), :].T
             waves = jnp.concatenate([waves[:mid], waves[mid:]], 1)

time: 139 us -> 126 us (0.906)
  Pallas kernels: 134 us -> 121 us
    pallas_call x1, Pallas kernels: 134 us -> 121 us  [kernel_body(): pl.pallas_call(solve_kernel, out_shape=jax.ShapeDtypeStruct(density.shape...]
where the time goes in v4:
time: 126 us
  Pallas kernels  121 us (96%)
  local copies, waits for them, and re-layouts  4.51 us (4%)
    pallas_call x1, Pallas kernels, kernel_body(): pl.pallas_call(solve_kernel, out_shape=jax.ShapeDtypeStruct(density.shape...  121 us
    unnamed x4, local copies, waits for them, and re-layouts  2.91 us

profile of v4, /device:TPU:0, one launch (start us, length us, event | category | flops | bytes accessed | tf_op | source)
XLA Modules:
  0.0 125.6 jit_solution(12687722819087067749)
XLA Ops:
  0.0 0.0 slice-start
  0.0 0.9 slice-done
  0.9 0.0 copy-start
  0.9 0.1 copy.11
  1.0 0.5 copy-done
  1.6 0.1 multiply_bitcast_fusion
  1.7 0.7 pad.4.factors
  2.4 121.0 %shard_map.91 = f32[2,32,32,128]{3,2,1,0:T(8,128)} custom-call(f32[2,32,32,128]{3,2,1,0:T(8,128)} %dens.1, f32[3,128,128]{2,1,0:T(8,128)} %pad.4.factors, bf16[256,384]{1,0:T(8,128)(2,1)} %constant.18.clone.fwd_z, bf16[256,384]{1,0:T(8,128)(2,1)} %constant.19.clone.fwd_y, bf16[384,256]{1,0:T(8,128)(2,1)} %constant.20.clone.fwd_x, ...), custom_call_target="tpu_custom_call" | custom-call | tf_op jit(solution)/shard_map/pallas_call | solution.py:313
  123.4 2.3 %copy.13 = f32[2,32,32,128]{3,2,1,0:T(8,128)} copy(f32[2,32,32,128]{3,2,1,0:T(8,128)} %shard_map.91) | data formatting | bytes 2097152
Async XLA Ops:
  0.0 0.9 slice-start
  0.9 0.7 copy-start
